TPU v7x, 128 devices: a whole 4x4x4 slice. The times are simulated.
128 devices in a mesh: dp: 64 (over z, y, x), cp: 2 (over core).
Axes of the slice: x: 4, y: 4, z: 4, core: 2. Of those that a mesh axis runs over, the one named last changes fastest.
Arguments:
- hidden_states: bfloat16 [64, 512, 3072], P('dp', 'cp')
- norm_gain: float32 [3072], replicated
- w_gate: bfloat16 [3072, 8192], replicated
- w_up: bfloat16 [3072, 8192], replicated
- w_down: bfloat16 [8192, 3072], replicated
- final_gain: float32 [3072], replicated
- w_value: float32 [3072], replicated
- b_value: float32 [], replicated
- rewards: float32 [64, 512], P('dp', 'cp')
- mask: int32 [64, 512], P('dp', 'cp')
Outputs:
- output 1: float32 [64, 512], P('dp', 'cp')
- output 2: float32 [64, 512], P('dp', 'cp')
- output 3: float32 [64, 512], P('dp', 'cp')
All inputs are finite; a program needn't handle non-finite values.
Results may differ from a plain program's by a relative error of at most 0.001.
Values sent between devices are 32-bit elements.
A program may use at most 1 GiB of HBM per device.

v0:
```python
import math
import jax
import jax.numpy as jnp
from jax import lax
from jax.sharding import PartitionSpec as P

NORM_EPS = 1e-6
WHITEN_EPS = 1e-8
DISCOUNT = 1.0
GAE_LAMBDA = 0.995
LOG_DECAY = math.log(DISCOUNT * GAE_LAMBDA)


def critic_values(x_blk, norm_gain, w_gate, w_up, w_down, final_gain, w_value, b_value):
    x_f32 = x_blk.astype(jnp.float32)
    normed = (x_f32 * lax.rsqrt(jnp.mean(x_f32 * x_f32, axis=-1, keepdims=True) + NORM_EPS) * norm_gain).astype(jnp.bfloat16)
    gate = jnp.einsum('bsd,df->bsf', normed, w_gate, preferred_element_type=jnp.float32)
    up_val = jnp.einsum('bsd,df->bsf', normed, w_up, preferred_element_type=jnp.float32)
    hidden = (jax.nn.silu(gate) * up_val).astype(jnp.bfloat16)
    resid = x_f32 + jnp.einsum('bsf,fd->bsd', hidden, w_down, preferred_element_type=jnp.float32)
    resid_n = resid * lax.rsqrt(jnp.mean(resid * resid, axis=-1, keepdims=True) + NORM_EPS)
    return jnp.sum(resid_n * (final_gain * w_value), axis=-1) + b_value


def decay_matrix(seq_len):
    positions = jnp.arange(seq_len)
    gap = positions[:, None] - positions[None, :]
    return jnp.where(gap >= 0, jnp.exp(jnp.maximum(gap, 0).astype(jnp.float32) * LOG_DECAY), 0.0)


def tail_decay(seq_len):
    positions = jnp.arange(seq_len)
    return jnp.exp((seq_len - positions).astype(jnp.float32) * LOG_DECAY)


def solution(mesh):
    cp_size = mesh.shape['cp']
    left_perm = [(source, source - 1) for source in range(1, cp_size)]

    def local_step(x_blk, norm_gain, w_gate, w_up, w_down, final_gain, w_value, b_value, rew_blk, mask_blk):
        row_count, seq_len = rew_blk.shape
        mask_f = mask_blk.astype(jnp.float32)
        values = mask_f * critic_values(x_blk, norm_gain, w_gate, w_up, w_down, final_gain, w_value, b_value)
        next_first = lax.ppermute(values[:, 0], 'cp', left_perm)
        next_vals = jnp.concatenate([values[:, 1:], next_first[:, None]], axis=1)
        delta = mask_f * rew_blk + DISCOUNT * next_vals - values
        local_adv = jnp.dot(delta, decay_matrix(seq_len), precision=lax.Precision.HIGHEST)
        head_adv = local_adv[:, 0]
        piece_gain = math.exp(seq_len * LOG_DECAY)

        def carry_step(step_idx, carry):
            return lax.ppermute(head_adv + piece_gain * carry, 'cp', left_perm)

        carry_in = lax.fori_loop(0, cp_size - 1, carry_step, jnp.zeros((row_count,), jnp.float32))
        advantage = local_adv + carry_in[:, None] * tail_decay(seq_len)[None, :]
        local_sums = jnp.stack([jnp.sum(mask_f), jnp.sum(mask_f * advantage), jnp.sum(mask_f * advantage * advantage)])
        totals = lax.psum(local_sums, ('dp', 'cp'))
        mean_adv = totals[1] / totals[0]
        var_adv = totals[2] / totals[0] - mean_adv * mean_adv
        white = mask_f * (advantage - mean_adv) * lax.rsqrt(var_adv + WHITEN_EPS)
        return values, mask_f * (advantage + values), white

    tok_spec = P('dp', 'cp')
    in_specs = (P('dp', 'cp', None), P(None), P(None, None), P(None, None), P(None, None), P(None), P(None), P(), tok_spec, tok_spec)
    return jax.shard_map(local_step, mesh=mesh, in_specs=in_specs, out_specs=(tok_spec, tok_spec, tok_spec), check_vma=False)
```

profile of v0, /device:TPU:1, one launch (start us, length us, event | category | flops | bytes accessed | tf_op | source)
XLA Modules:
  0.0 160.6 jit_solution(13234401470508760767)
XLA Ops:
  0.6 1.8 %fusion.7 = f32[256]{0:T(256)S(1)} fusion(bf16[1,256,3072]{2,1,0:T(8,128)(2,1)} %param.10), kind=kLoop, calls=%fused_computation.11 | loop fusion | flops 2359040 | bytes 1573888 | tf_op jit(solution)/shard_map/reduce_sum | solution.py:16
  2.4 0.0 copy-start
  2.4 0.0 copy-start.5
  2.5 25.0 %fusion.13 = f32[256,8192]{1,0:T(8,128)} fusion(bf16[3072,8192]{1,0:T(8,128)(2,1)} %param.12, bf16[1,256,3072]{2,1,0:T(8,128)(2,1)} %param.10, f32[3072]{0:T(1024)} %param.11, f32[256]{0:T(256)S(1)} %add_rsqrt_fusion.1), kind=kOutput, calls=%fused_computation.17 | convolution fusion | flops 12888047616 | bytes 60306432 | tf_op jit(solution)/shard_map/bsd,df->bsf/dot_general | solution.py:17
  27.5 0.0 copy-done
  27.5 0.0 copy-done.5
  27.5 24.4 %fusion.clone.5.clone.4 = bf16[256,8192]{1,0:T(8,128)(2,1)} fusion(bf16[3072,8192]{1,0:T(8,128)(2,1)} %param.13, f32[256,8192]{1,0:T(8,128)} %fusion.13, bf16[1,256,3072]{2,1,0:T(8,128)(2,1)S(1)} %copy-done, f32[3072]{0:T(1024)S(1)} %copy-done.5, f32[256]{0:T(256)S(1)} %add_rsqrt_fusion.1), kind=kOutput, calls=%fused_computation.1.clone.clone.clone.clone.clone.clone.clone.clone.clone.1 | convolution fusion | flops 12900630528 | bytes 64500736 | tf_op jit(solution)/shard_map/bsd,df->bsf/dot_general | solution.py:18
  51.9 0.0 copy-start.1
  51.9 0.0 copy-start.2
  51.9 22.3 %multiply_reduce_fusion.1 = (f32[256]{0:T(256)S(1)}, f32[1,256,3072]{2,1,0:T(8,128)S(1)}) fusion(bf16[8192,3072]{1,0:T(8,128)(2,1)} %param.14, bf16[1,256,3072]{2,1,0:T(8,128)(2,1)} %param.10, bf16[256,8192]{1,0:T(8,128)(2,1)} %fusion.clone.5.clone.4), kind=kOutput, calls=%fused_computation.15 | convolution fusion | flops 12888047616 | bytes 59245568 | tf_op jit(solution)/shard_map/bsf,fd->bsd/dot_general | solution.py:20
  74.1 0.0 copy-start.3
  74.2 0.0 copy-start.6
  74.8 0.0 copy-done.1
  74.8 0.0 copy-done.2
  74.9 0.5 multiply_reduce_fusion
  75.3 0.0 copy-done.3
  75.4 0.0 copy-start.4
  75.4 0.5 slice.26
  75.9 3.8 %collective-permute-start = (f32[1]{0:T(128)}, f32[1]{0:T(128)}, u32[]{:S(2)}, u32[]{:S(2)}) collective-permute-start(f32[1]{0:T(128)} %bitcast.3), channel_id=1, source_target_pairs={{1,0},{3,2},{5,4},{7,6},{9,8},{11,10},{13,12},{15,14},{17,16},{19,... | collective-permute-start | bytes 20 | tf_op jit(solution)/shard_map/ppermute | solution.py:44
  79.7 0.1 slice.25
  79.8 0.1 collective-permute-done
  79.9 0.0 copy-done.6
  80.0 0.9 fusion.21
  80.9 0.6 slice.27
  81.4 2.8 %collective-permute-start.1 = (f32[1]{0:T(128)}, f32[1]{0:T(128)}, u32[]{:S(2)}, u32[]{:S(2)}) collective-permute-start(f32[1]{0:T(128)} %bitcast.8), channel_id=1, source_target_pairs={{1,0},{3,2},{5,4},{7,6},{9,8},{11,10},{13,12},{15,14},{17,16},{19,... | collective-permute-start | bytes 20 | tf_op jit(solution)/shard_map/while/body/eval_jaxpr/ppermute | solution.py:52
  84.2 0.2 collective-permute-done.1
  84.4 0.7 multiply_add_fusion
  85.1 1.2 fusion.35
  86.3 1.9 %pad_maximum_fusion = f32[3]{0:T(128)S(1)} fusion(f32[1]{0:T(128)} %bitcast.13, f32[1]{0:T(128)} %bitcast.12, f32[1]{0:T(128)} %bitcast.11), kind=kLoop, calls=%fused_computation.46 | loop fusion | flops 6 | bytes 24 | tf_op jit(solution)/shard_map/stack | solution.py:56
  88.2 68.0 %psum.7 = f32[3]{0:T(128)S(1)} all-reduce(f32[3]{0:T(128)S(1)} %pad_maximum_fusion), channel_id=1, replica_groups=mesh['dp'=64,'cp'=2] {'dp','cp'}, use_global_device_ids=true, to_apply=%region_6.7 | all-reduce | flops 3 | bytes 24 | tf_op jit(solution)/shard_map/psum | solution.py:57
  156.2 0.6 fusion.41
  158.1 0.7 broadcast_subtract_fusion
  160.1 0.6 multiply_multiply_fusion
  160.6 0.0 copy-done.4
  (5 shorter events, 0.0 us)
Async XLA Ops:
  2.4 25.0 %copy-start = (bf16[1,256,3072]{2,1,0:T(8,128)(2,1)S(1)}, bf16[1,256,3072]{2,1,0:T(8,128)(2,1)}, u32[]{:S(2)}) copy-start(bf16[1,256,3072]{2,1,0:T(8,128)(2,1)} %param.10) | copy-start | bytes 4718596
  2.4 25.0 %copy-start.5 = (f32[3072]{0:T(1024)S(1)}, f32[3072]{0:T(1024)}, u32[]{:S(2)}) copy-start(f32[3072]{0:T(1024)} %param.11) | copy-start | bytes 36868
  51.9 23.0 %copy-start.1 = (f32[3072]{0:T(1024)S(1)}, f32[3072]{0:T(1024)}, u32[]{:S(2)}) copy-start(f32[3072]{0:T(1024)} %param.15) | copy-start | bytes 36868
  51.9 23.0 %copy-start.2 = (f32[3072]{0:T(1024)S(1)}, f32[3072]{0:T(1024)}, u32[]{:S(2)}) copy-start(f32[3072]{0:T(1024)} %param.16) | copy-start | bytes 36868
  74.1 1.2 copy-start.3
  74.2 5.8 %copy-start.6 = (f32[1,256]{1,0:T(1,128)S(1)}, f32[1,256]{1,0:T(1,128)}, u32[]{:S(2)}) copy-start(f32[1,256]{1,0:T(1,128)} %param.18) | copy-start | bytes 3076
  75.4 85.3 %copy-start.4 = (f32[1,256]{1,0:T(1,128)}, f32[1,256]{1,0:T(1,128)S(1)}, u32[]{:S(2)}) copy-start(f32[1,256]{1,0:T(1,128)S(1)} %convert_multiply_fusion.3) | copy-start | bytes 3076
  75.9 4.1 %collective-permute-start = (f32[1]{0:T(128)}, f32[1]{0:T(128)}, u32[]{:S(2)}, u32[]{:S(2)}) collective-permute-start(f32[1]{0:T(128)} %bitcast.3), channel_id=1, source_target_pairs={{1,0},{3,2},{5,4},{7,6},{9,8},{11,10},{13,12},{15,14},{17,16},{19,... | collective-permute-start | bytes 20 | tf_op jit(solution)/shard_map/ppermute | solution.py:44
  81.4 3.0 %collective-permute-start.1 = (f32[1]{0:T(128)}, f32[1]{0:T(128)}, u32[]{:S(2)}, u32[]{:S(2)}) collective-permute-start(f32[1]{0:T(128)} %bitcast.8), channel_id=1, source_target_pairs={{1,0},{3,2},{5,4},{7,6},{9,8},{11,10},{13,12},{15,14},{17,16},{19,... | collective-permute-start | bytes 20 | tf_op jit(solution)/shard_map/while/body/eval_jaxpr/ppermute | solution.py:52
where the time goes:
time: 161 us
  matrix products  72.6 us (45%)
  blocking collectives  68 us (42%)
  other arithmetic  7.38 us (5%)
  starting transfers between devices  6.61 us (4%)
  between operations  3.93 us (2%)
  local copies, waits for them, and re-layouts  1.79 us (1%)
    psum x1, blocking collectives, local_step(): totals = lax.psum(local_sums, ('dp', 'cp'))  68 us
    dot_general x1, matrix products, critic_values(): jnp.einsum('bsd,df->bsf', normed, w_gate, preferred_element_type=jnp.floa...  25 us
    dot_general x1, matrix products, critic_values(): jnp.einsum('bsd,df->bsf', normed, w_up, preferred_element_type=jnp.float32)  24.4 us
    dot_general x1, matrix products, critic_values(): jnp.einsum('bsf,fd->bsd', hidden, w_down, preferred_element_type=jnp.floa...  22.3 us
    ppermute x1, starting transfers between devices, local_step(): next_first = lax.ppermute(values[:, 0], 'cp', left_perm)  3.83 us
  transfers between devices with their start and end apart: 2, of which 2 were waited for; matrix products, arithmetic and copies ran while one was open for 0% of the time, Pallas kernels for 0%

commit v1 on v0

v1 whole, which is shorter than its diff:
```python
import functools
import math

import jax
import jax.numpy as jnp
from jax import lax
from jax.experimental import pallas as pl
from jax.experimental.pallas import tpu as pltpu
from jax.sharding import PartitionSpec as P

NORM_EPS = 1e-6
WHITEN_EPS = 1e-8
DISCOUNT = 1.0
GAE_LAMBDA = 0.995
DECAY = DISCOUNT * GAE_LAMBDA
LOG_DECAY = math.log(DECAY)
MESH = pl.DeviceIdType.MESH


def critic_values(x_blk, norm_gain, w_gate, w_up, w_down, final_gain, w_value, b_value):
    x_f32 = x_blk.astype(jnp.float32)
    normed = (x_f32 * lax.rsqrt(jnp.mean(x_f32 * x_f32, axis=-1, keepdims=True) + NORM_EPS) * norm_gain).astype(jnp.bfloat16)
    gate = jnp.einsum('bsd,df->bsf', normed, w_gate, preferred_element_type=jnp.float32)
    up_val = jnp.einsum('bsd,df->bsf', normed, w_up, preferred_element_type=jnp.float32)
    hidden = (jax.nn.silu(gate) * up_val).astype(jnp.bfloat16)
    resid = x_f32 + jnp.einsum('bsf,fd->bsd', hidden, w_down, preferred_element_type=jnp.float32)
    resid_n = resid * lax.rsqrt(jnp.mean(resid * resid, axis=-1, keepdims=True) + NORM_EPS)
    return jnp.sum(resid_n * (final_gain * w_value), axis=-1) + b_value


def greet(dp_size):
    chip, core = lax.axis_index("dp"), lax.axis_index("cp")
    barrier = pltpu.get_barrier_semaphore()
    pl.semaphore_signal(barrier, inc=1, device_id=(chip, 1 - core), device_id_type=MESH)

    def tell(k, _):
        pl.semaphore_signal(barrier, inc=1, device_id=(lax.rem(chip + k, dp_size), core), device_id_type=MESH)
        return 0

    lax.fori_loop(1, dp_size, tell, 0)


def await_greetings(dp_size):
    pl.semaphore_wait(pltpu.get_barrier_semaphore(), dp_size)


def positions(n):
    row = lax.broadcasted_iota(jnp.int32, (n, n), 0)
    col = lax.broadcasted_iota(jnp.int32, (n, n), 1)
    return row, col


def column_of(row_vec, n):
    row, col = positions(n)
    return jnp.sum(jnp.where(row == col, row_vec, 0.0), axis=1, keepdims=True)


def reward_part(rew_col, n):
    row, col = positions(n)
    gap = row - col
    decay = jnp.where(gap >= 0, jnp.exp(jnp.maximum(gap, 0).astype(jnp.float32) * LOG_DECAY), 0.0)
    return jnp.sum(decay * rew_col, axis=0, keepdims=True)


def value_weights(n):
    row, col = positions(n)
    gap = row - col
    later = DISCOUNT * (1.0 - GAE_LAMBDA) * jnp.exp(jnp.maximum(gap - 1, 0).astype(jnp.float32) * LOG_DECAY)
    return jnp.where(gap > 0, later, jnp.where(gap == 0, -1.0, 0.0))


def finish(dp_size, v_col, reward_row, weights, mask_row, values_ref, returns_ref, white_ref,
           mine, theirs, total, gathered, pair_send, pair_recv, all_send, all_recv):
    n = mask_row.shape[1]
    chip, core = lax.axis_index("dp"), lax.axis_index("cp")
    row, col = positions(n)
    adv = reward_row + jnp.sum(weights * v_col, axis=0, keepdims=True)
    v_row = jnp.sum(jnp.where(row == col, v_col, 0.0), axis=0, keepdims=True)
    ahead = (n - 1) - lax.broadcasted_iota(jnp.int32, (1, n), 1)
    reach = jnp.exp(ahead.astype(jnp.float32) * LOG_DECAY)
    madv, mreach = mask_row * adv, mask_row * reach

    def add_up(a):
        return jnp.sum(a, axis=1, keepdims=True)

    carry_out = DISCOUNT * v_row[:, 0:1] + DECAY * adv[:, 0:1]
    parts = [add_up(mask_row), add_up(madv), add_up(madv * adv), add_up(mreach), add_up(mreach * adv), add_up(mreach * reach), carry_out]
    lane = lax.broadcasted_iota(jnp.int32, (1, 128), 1)
    packed = jnp.zeros((1, 128), jnp.float32)
    for place, part in enumerate(parts):
        packed = jnp.where(lane == place, part, packed)
    mine[...] = packed
    pair = pltpu.make_async_remote_copy(src_ref=mine, dst_ref=theirs, send_sem=pair_send, recv_sem=pair_recv,
                                        device_id=(chip, 1 - core), device_id_type=MESH)
    pair.start()
    pair.wait()
    other = theirs[...]
    is_left = core == 0
    left, right = jnp.where(is_left, packed, other), jnp.where(is_left, other, packed)
    carry = right[:, 6:7]
    count = left[:, 0:1] + right[:, 0:1]
    first = left[:, 1:2] + right[:, 1:2] + carry * left[:, 3:4]
    second = left[:, 2:3] + right[:, 2:3] + carry * (2.0 * left[:, 4:5] + carry * left[:, 5:6])
    own = jnp.where(lane == 0, count, jnp.where(lane == 1, first, jnp.where(lane == 2, second, 0.0)))
    total[...] = own

    def push(k, _):
        pltpu.make_async_remote_copy(
            src_ref=total, dst_ref=gathered.at[pl.ds(k - 1, 1)], send_sem=all_send, recv_sem=all_recv,
            device_id=(lax.rem(chip + k, dp_size), core), device_id_type=MESH).start()
        return 0

    lax.fori_loop(1, dp_size, push, 0)
    adv = adv + jnp.where(is_left, carry, 0.0) * reach
    values_ref[...] = v_row
    returns_ref[...] = mask_row * (adv + v_row)
    everything = pltpu.make_async_remote_copy(src_ref=gathered, dst_ref=gathered, send_sem=all_send, recv_sem=all_recv,
                                              device_id=(chip, 1 - core), device_id_type=MESH)
    everything.wait_recv()
    sums = own + jnp.sum(gathered[...], axis=0, keepdims=True)
    count, first, second = sums[:, 0:1], sums[:, 1:2], sums[:, 2:3]
    mean = first / count
    var = second / count - mean * mean
    white_ref[...] = mask_row * (adv - mean) * lax.rsqrt(var + WHITEN_EPS)
    everything.wait_send()


def tail_kernel(dp_size, v_ref, rew_ref, mask_ref, values_ref, returns_ref, white_ref, *scratch):
    n = v_ref.shape[1]
    greet(dp_size)
    mask_row = mask_ref[...].astype(jnp.float32)
    reward_row = reward_part(column_of(mask_row * rew_ref[...], n), n)
    v_col = column_of(mask_row * v_ref[...], n)
    await_greetings(dp_size)
    finish(dp_size, v_col, reward_row, value_weights(n), mask_row, values_ref, returns_ref, white_ref, *scratch)


def finish_scratch(dp_size):
    return [
        pltpu.VMEM((1, 128), jnp.float32),
        pltpu.VMEM((1, 128), jnp.float32),
        pltpu.VMEM((1, 128), jnp.float32),
        pltpu.VMEM((dp_size - 1, 128), jnp.float32),
        pltpu.SemaphoreType.DMA,
        pltpu.SemaphoreType.DMA,
        pltpu.SemaphoreType.DMA,
        pltpu.SemaphoreType.DMA,
    ]


def solution(mesh):
    dp_size = mesh.shape['dp']

    def local_step(x_blk, norm_gain, w_gate, w_up, w_down, final_gain, w_value, b_value, rew_blk, mask_blk):
        v = critic_values(x_blk, norm_gain, w_gate, w_up, w_down, final_gain, w_value, b_value)
        row = jax.ShapeDtypeStruct(rew_blk.shape, jnp.float32)
        vmem = pl.BlockSpec(memory_space=pltpu.VMEM)
        return pl.pallas_call(
            functools.partial(tail_kernel, dp_size),
            out_shape=(row, row, row),
            in_specs=[vmem] * 3,
            out_specs=(vmem,) * 3,
            scratch_shapes=finish_scratch(dp_size),
            compiler_params=pltpu.CompilerParams(collective_id=0, has_side_effects=True),
        )(v, rew_blk, mask_blk)

    tok_spec = P('dp', 'cp')
    in_specs = (P('dp', 'cp', None), P(None), P(None, None), P(None, None), P(None, None), P(None), P(None), P(), tok_spec, tok_spec)
    return jax.shard_map(local_step, mesh=mesh, in_specs=in_specs, out_specs=(tok_spec, tok_spec, tok_spec), check_vma=False)
```

time: 161 us -> 96.9 us (0.60)
  blocking collectives: 68 us -> 0 us
  Pallas kernels: 0 us -> 17.4 us
  starting transfers between devices: 6.61 us -> 0 us
  other arithmetic: 7.38 us -> 2.86 us
  between operations: 3.93 us -> 1.36 us
  local copies, waits for them, and re-layouts: 1.79 us -> 3.7 us
    psum x1 -> x0, blocking collectives: 68 us -> none  [local_step(): totals = lax.psum(local_sums, ('dp', 'cp'))]
    pallas_call x0 -> x1, Pallas kernels: none -> 17.4 us  [local_step(): pl.pallas_call(functools.partial(tail_kernel, dp_size), out_shape=(row, r...]
    ppermute x2 -> x0, starting transfers between devices: 6.61 us -> none  [the longest x1 3.83 us: local_step(): next_first = lax.ppermute(values[:, 0], 'cp', left_perm)]
    unnamed x14 -> x11, local copies, waits for them, and re-layouts: 0.04 us -> 3.7 us
    another operation x1 -> x0, other arithmetic: 1.91 us -> none  [local_step(): jnp.stack([jnp.sum(mask_f), jnp.sum(mask_f * advantage), jnp.sum(mask_f *...]
    slice x4 -> x0, local copies, waits for them, and re-layouts: 1.76 us -> none  [the longest x1 0.61 us: local_step(): var_adv = totals[2] / totals[0] - mean_adv * mean_adv]
  transfers between devices with their start and end apart: 2 -> 0, of which waited for: 2 -> 0; matrix products, arithmetic and copies ran while one was open for 0% -> 0% of each run, Pallas kernels for 0% -> 0%
where the time goes in v1:
time: 96.9 us; the launch traced here: 96.7 us
  matrix products  71.3 us (74%)
  Pallas kernels  17.4 us (18%)
  local copies, waits for them, and re-layouts  3.7 us (4%)
  other arithmetic  2.86 us (3%)
  between operations  1.36 us (1%)
    dot_general x1, matrix products, critic_values(): jnp.einsum('bsd,df->bsf', normed, w_gate, preferred_element_type=jnp.floa...  25 us
    dot_general x1, matrix products, critic_values(): jnp.einsum('bsd,df->bsf', normed, w_up, preferred_element_type=jnp.float32)  24.3 us
    dot_general x1, matrix products, critic_values(): jnp.einsum('bsf,fd->bsd', hidden, w_down, preferred_element_type=jnp.floa...  22 us
    pallas_call x1, Pallas kernels, local_step(): pl.pallas_call(functools.partial(tail_kernel, dp_size), out_shape=(row, r...  17.4 us
    unnamed x11, local copies, waits for them, and re-layouts  3.7 us

profile of v1, /device:TPU:1, one launch (start us, length us, event | category | flops | bytes accessed | tf_op | source)
XLA Modules:
  0.0 96.7 jit_solution(8202172291253816915)
XLA Ops:
  0.6 1.8 %fusion.7 = f32[256]{0:T(256)S(1)} fusion(bf16[1,256,3072]{2,1,0:T(8,128)(2,1)} %param.10), kind=kLoop, calls=%fused_computation.11 | loop fusion | flops 2359040 | bytes 1573888 | tf_op jit(solution)/shard_map/reduce_sum | solution.py:22
  2.4 0.0 copy-start
  2.4 0.0 copy-start.3
  2.5 25.0 %fusion.13 = f32[256,8192]{1,0:T(8,128)} fusion(bf16[3072,8192]{1,0:T(8,128)(2,1)} %param.12, bf16[1,256,3072]{2,1,0:T(8,128)(2,1)} %param.10, f32[3072]{0:T(1024)} %param.11, f32[256]{0:T(256)S(1)} %add_rsqrt_fusion.1), kind=kOutput, calls=%fused_computation.17 | convolution fusion | flops 12888047616 | bytes 60306432 | tf_op jit(solution)/shard_map/bsd,df->bsf/dot_general | solution.py:23
  27.5 0.0 copy-done
  27.5 0.0 copy-done.3
  27.5 24.3 %fusion.clone.5.clone.4 = bf16[256,8192]{1,0:T(8,128)(2,1)} fusion(bf16[3072,8192]{1,0:T(8,128)(2,1)} %param.13, f32[256,8192]{1,0:T(8,128)} %fusion.13, bf16[1,256,3072]{2,1,0:T(8,128)(2,1)S(1)} %copy-done, f32[3072]{0:T(1024)S(1)} %copy-done.3, f32[256]{0:T(256)S(1)} %add_rsqrt_fusion.1), kind=kOutput, calls=%fused_computation.1.clone.clone.clone.clone.clone.clone.clone.clone.clone.1 | convolution fusion | flops 12900630528 | bytes 64500736 | tf_op jit(solution)/shard_map/bsd,df->bsf/dot_general | solution.py:24
  51.8 0.0 copy-start.1
  51.8 0.0 copy-start.2
  51.8 22.0 %multiply_reduce_fusion.1 = (f32[256]{0:T(256)S(1)}, f32[1,256,3072]{2,1,0:T(8,128)S(1)}) fusion(bf16[8192,3072]{1,0:T(8,128)(2,1)} %param.14, bf16[1,256,3072]{2,1,0:T(8,128)(2,1)S(1)} %copy-done, bf16[256,8192]{1,0:T(8,128)(2,1)} %fusion.clone.5.clone.4), kind=kOutput, calls=%fused_computation.15 | convolution fusion | flops 12888047616 | bytes 59245568 | tf_op jit(solution)/shard_map/bsf,fd->bsd/dot_general | solution.py:26
  73.8 0.0 copy-done.1
  73.8 0.0 copy-done.2
  73.8 0.5 multiply_reduce_fusion
  75.0 0.6 broadcast_add_fusion
  75.5 17.4 %shard_map.121 = (f32[1,256]{1,0:T(1,128)}, f32[1,256]{1,0:T(1,128)}, f32[1,256]{1,0:T(1,128)}) custom-call(f32[1,256]{1,0:T(1,128)} %bitcast.23, f32[1,256]{1,0:T(1,128)} %rew_ref.1, s32[1,256]{1,0:T(1,128)} %mask_ref.1), custom_call_target="tpu_custom_call" | custom-call | tf_op jit(solution)/shard_map/pallas_call | solution.py:158
  93.0 1.2 %copy.17 = f32[1,256]{1,0:T(1,128)} copy(f32[1,256]{1,0:T(1,128)} %get-tuple-element.8) | data formatting | bytes 2048
  94.2 1.2 %copy.18 = f32[1,256]{1,0:T(1,128)} copy(f32[1,256]{1,0:T(1,128)} %get-tuple-element.9) | data formatting | bytes 2048
  95.4 1.2 %copy.19 = f32[1,256]{1,0:T(1,128)} copy(f32[1,256]{1,0:T(1,128)} %get-tuple-element.10) | data formatting | bytes 2048
  (3 shorter events, 0.0 us)
Async XLA Ops:
  2.4 25.0 %copy-start = (bf16[1,256,3072]{2,1,0:T(8,128)(2,1)S(1)}, bf16[1,256,3072]{2,1,0:T(8,128)(2,1)}, u32[]{:S(2)}) copy-start(bf16[1,256,3072]{2,1,0:T(8,128)(2,1)} %param.10) | copy-start | bytes 4718596
  2.4 25.0 %copy-start.3 = (f32[3072]{0:T(1024)S(1)}, f32[3072]{0:T(1024)}, u32[]{:S(2)}) copy-start(f32[3072]{0:T(1024)} %param.11) | copy-start | bytes 36868
  51.8 22.0 %copy-start.1 = (f32[3072]{0:T(1024)S(1)}, f32[3072]{0:T(1024)}, u32[]{:S(2)}) copy-start(f32[3072]{0:T(1024)} %param.15) | copy-start | bytes 36868
  51.8 22.0 %copy-start.2 = (f32[3072]{0:T(1024)S(1)}, f32[3072]{0:T(1024)}, u32[]{:S(2)}) copy-start(f32[3072]{0:T(1024)} %param.16) | copy-start | bytes 36868

commit v2 on v1

--- a/solution.py
+++ b/solution.py
@@ -17,15 +17,114 @@
 MESH = pl.DeviceIdType.MESH
 
 
-def critic_values(x_blk, norm_gain, w_gate, w_up, w_down, final_gain, w_value, b_value):
-    x_f32 = x_blk.astype(jnp.float32)
-    normed = (x_f32 * lax.rsqrt(jnp.mean(x_f32 * x_f32, axis=-1, keepdims=True) + NORM_EPS) * norm_gain).astype(jnp.bfloat16)
-    gate = jnp.einsum('bsd,df->bsf', normed, w_gate, preferred_element_type=jnp.float32)
-    up_val = jnp.einsum('bsd,df->bsf', normed, w_up, preferred_element_type=jnp.float32)
-    hidden = (jax.nn.silu(gate) * up_val).astype(jnp.bfloat16)
-    resid = x_f32 + jnp.einsum('bsf,fd->bsd', hidden, w_down, preferred_element_type=jnp.float32)
-    resid_n = resid * lax.rsqrt(jnp.mean(resid * resid, axis=-1, keepdims=True) + NORM_EPS)
-    return jnp.sum(resid_n * (final_gain * w_value), axis=-1) + b_value
+TILE = 256
+WIDE = 512
+DEPTH2 = 2048
+S1, S2 = 4, 8
+NT = 512
+
+
+def silu_mul(g, u):
+    return (g * (1.0 / (1.0 + jnp.exp(-g))) * u).astype(jnp.bfloat16)
+
+
+def mlp(x_hbm, wg_hbm, wu_hbm, wd_hbm, g2_ref, gf_ref, wv_ref,
+        x_buf, n_buf, u_buf, wg_ring, wu_ring, wd_ring, sq_acc, hd_acc, h_buf, x_sem, g_sem, u_sem, d_sem, while_loading):
+    rows, model = x_buf.shape
+    ffn = u_buf.shape[1]
+    n1 = ffn // WIDE
+    per_out = ffn // DEPTH2
+    n_out = model // WIDE
+    n2 = n_out * per_out
+    k1, k2 = model // TILE, DEPTH2 // TILE
+
+    def g_copy(i):
+        s = lax.rem(i, S1)
+        return pltpu.make_async_copy(wg_hbm.at[:, pl.ds(pl.multiple_of(i * WIDE, WIDE), WIDE)], wg_ring.at[s], g_sem.at[s])
+
+    def u_copy(i):
+        s = lax.rem(i, S1)
+        return pltpu.make_async_copy(wu_hbm.at[:, pl.ds(pl.multiple_of(i * WIDE, WIDE), WIDE)], wu_ring.at[s], u_sem.at[s])
+
+    def d_copy(p):
+        s = lax.rem(p, S2)
+        o, kk = p // per_out, lax.rem(p, per_out)
+        return pltpu.make_async_copy(
+            wd_hbm.at[pl.ds(pl.multiple_of(kk * DEPTH2, DEPTH2), DEPTH2), pl.ds(pl.multiple_of(o * WIDE, WIDE), WIDE)],
+            wd_ring.at[s], d_sem.at[s])
+
+    x_copy = pltpu.make_async_copy(x_hbm, x_buf, x_sem)
+    x_copy.start()
+    for i in range(S1):
+        g_copy(i).start()
+        u_copy(i).start()
+    while_loading()
+    x_copy.wait()
+
+    def norm(b, _):
+        r = pl.ds(pl.multiple_of(b * 32, 32), 32)
+        xf = x_buf[r, :].astype(jnp.float32)
+        scale = lax.rsqrt(jnp.mean(xf * xf, axis=1, keepdims=True) + NORM_EPS)
+        n_buf[r, :] = (xf * scale * g2_ref[...]).astype(jnp.bfloat16)
+        return 0
+    lax.fori_loop(0, rows // 32, norm, 0)
+    sq_acc[...] = jnp.zeros_like(sq_acc)
+    hd_acc[...] = jnp.zeros_like(hd_acc)
+
+    def dot(a, b):
+        return jnp.dot(a, b, preferred_element_type=jnp.float32)
+
+    def issue1(i):
+        @pl.when(i + S1 < n1)
+        def _():
+            g_copy(i + S1).start()
+            u_copy(i + S1).start()
+
+        @pl.when(i + S1 >= n1)
+        def _():
+            first = (i + S1 - n1) * (S2 // S1)
+            for j in range(S2 // S1):
+                d_copy(first + j).start()
+
+    UN = 2
+    def loop1(b, _):
+        for j in range(UN):
+            i = b * UN + j
+            slot = lax.rem(i, S1)
+            g_copy(i).wait()
+            u_copy(i).wait()
+            for half in range(WIDE // NT):
+                c = pl.ds(half * NT, NT)
+                g = dot(n_buf[...], wg_ring[slot, :, c])
+                u = dot(n_buf[...], wu_ring[slot, :, c])
+                u_buf[:, pl.ds(pl.multiple_of(i * WIDE + half * NT, NT), NT)] = silu_mul(g, u)
+        for j in range(UN):
+            issue1(b * UN + j)
+        return 0
+    lax.fori_loop(0, n1 // UN, loop1, 0)
+
+    def loop2(o, _):
+        h = None
+        for kk in range(per_out):
+            p = o * per_out + kk
+            slot = lax.rem(p, S2)
+            d_copy(p).wait()
+            part = dot(u_buf[:, pl.ds(kk * DEPTH2, DEPTH2)], wd_ring[slot])
+            if kk == 0:
+                h_buf[...] = part
+            elif kk < per_out - 1:
+                h_buf[...] += part
+            else:
+                for q in range(4):
+                    c = pl.ds(pl.multiple_of(o * WIDE + q * 128, 128), 128)
+                    h = x_buf[:, c].astype(jnp.float32) + (h_buf[:, q*128:(q+1)*128] + part[:, q*128:(q+1)*128])
+                    sq_acc[...] += h * h
+                    hd_acc[...] += h * (gf_ref[:, c] * wv_ref[:, c])
+            @pl.when(p + S2 < n2)
+            def _():
+                d_copy(p + S2).start()
+        return 0
+    lax.fori_loop(0, n_out, loop2, 0)
 
 
 def greet(dp_size):
@@ -69,7 +168,7 @@
     return jnp.where(gap > 0, later, jnp.where(gap == 0, -1.0, 0.0))
 
 
-def finish(dp_size, v_col, reward_row, weights, mask_row, values_ref, returns_ref, white_ref,
+def finish(dp_size, v_col, reward_row, weights, mask_row, out_ref,
            mine, theirs, total, gathered, pair_send, pair_recv, all_send, all_recv):
     n = mask_row.shape[1]
     chip, core = lax.axis_index("dp"), lax.axis_index("cp")
@@ -112,8 +211,8 @@
 
     lax.fori_loop(1, dp_size, push, 0)
     adv = adv + jnp.where(is_left, carry, 0.0) * reach
-    values_ref[...] = v_row
-    returns_ref[...] = mask_row * (adv + v_row)
+    out_ref[0:1, :] = v_row
+    out_ref[1:2, :] = mask_row * (adv + v_row)
     everything = pltpu.make_async_remote_copy(src_ref=gathered, dst_ref=gathered, send_sem=all_send, recv_sem=all_recv,
                                               device_id=(chip, 1 - core), device_id_type=MESH)
     everything.wait_recv()
@@ -121,18 +220,50 @@
     count, first, second = sums[:, 0:1], sums[:, 1:2], sums[:, 2:3]
     mean = first / count
     var = second / count - mean * mean
-    white_ref[...] = mask_row * (adv - mean) * lax.rsqrt(var + WHITEN_EPS)
+    out_ref[2:3, :] = mask_row * (adv - mean) * lax.rsqrt(var + WHITEN_EPS)
     everything.wait_send()
 
 
-def tail_kernel(dp_size, v_ref, rew_ref, mask_ref, values_ref, returns_ref, white_ref, *scratch):
-    n = v_ref.shape[1]
+def kernel(dp_size, x_hbm, wg, wu, wd, g2, gf, wv, bv, rew_ref, mask_ref, out_ref, weights_ref, reward_ref, *scratch):
+    n = rew_ref.shape[1]
+    mlp_scratch, tail_scratch = scratch[:13], scratch[13:]
     greet(dp_size)
+
+    def while_loading():
+        reward_ref[...] = reward_part(column_of(mask_ref[...].astype(jnp.float32) * rew_ref[...], n), n)
+        weights_ref[...] = value_weights(n)
+
+    mlp(x_hbm, wg, wu, wd, g2, gf, wv, *mlp_scratch, while_loading)
+    model = x_hbm.shape[1]
     mask_row = mask_ref[...].astype(jnp.float32)
-    reward_row = reward_part(column_of(mask_row * rew_ref[...], n), n)
-    v_col = column_of(mask_row * v_ref[...], n)
+    sq_acc, hd_acc = mlp_scratch[6], mlp_scratch[7]
+    square = jnp.sum(sq_acc[...], axis=1, keepdims=True)
+    head = jnp.sum(hd_acc[...], axis=1, keepdims=True)
+    v_col = column_of(mask_row, n) * (head * lax.rsqrt(square * (1.0 / model) + NORM_EPS) + bv[0])
     await_greetings(dp_size)
-    finish(dp_size, v_col, reward_row, value_weights(n), mask_row, values_ref, returns_ref, white_ref, *scratch)
+    finish(dp_size, v_col, reward_ref[...], weights_ref[...], mask_row, out_ref, *tail_scratch)
+
+
+def hand_out(packed_ref, values_ref, returns_ref, white_ref):
+    values_ref[...] = packed_ref[0:1, :]
+    returns_ref[...] = packed_ref[1:2, :]
+    white_ref[...] = packed_ref[2:3, :]
+
+
+def mlp_scratch_shapes(rows, model, ffn):
+    bf, f32, sem = jnp.bfloat16, jnp.float32, pltpu.SemaphoreType.DMA
+    return [
+        pltpu.VMEM((rows, model), bf),
+        pltpu.VMEM((rows, model), bf),
+        pltpu.VMEM((rows, ffn), bf),
+        pltpu.VMEM((S1, model, WIDE), bf),
+        pltpu.VMEM((S1, model, WIDE), bf),
+        pltpu.VMEM((S2, DEPTH2, WIDE), bf),
+        pltpu.VMEM((rows, 128), f32),
+        pltpu.VMEM((rows, 128), f32),
+        pltpu.VMEM((rows, WIDE), f32),
+        sem, sem((S1,)), sem((S1,)), sem((S2,)),
+    ]
 
 
 def finish_scratch(dp_size):
@@ -152,17 +283,22 @@
     dp_size = mesh.shape['dp']
 
     def local_step(x_blk, norm_gain, w_gate, w_up, w_down, final_gain, w_value, b_value, rew_blk, mask_blk):
-        v = critic_values(x_blk, norm_gain, w_gate, w_up, w_down, final_gain, w_value, b_value)
-        row = jax.ShapeDtypeStruct(rew_blk.shape, jnp.float32)
+        rows = rew_blk.shape[1]
+        model, ffn = w_gate.shape
+        hbm = pl.BlockSpec(memory_space=pl.ANY)
         vmem = pl.BlockSpec(memory_space=pltpu.VMEM)
-        return pl.pallas_call(
-            functools.partial(tail_kernel, dp_size),
-            out_shape=(row, row, row),
-            in_specs=[vmem] * 3,
-            out_specs=(vmem,) * 3,
-            scratch_shapes=finish_scratch(dp_size),
-            compiler_params=pltpu.CompilerParams(collective_id=0, has_side_effects=True),
-        )(v, rew_blk, mask_blk)
+        smem = pl.BlockSpec(memory_space=pltpu.SMEM)
+        packed = pl.pallas_call(
+            functools.partial(kernel, dp_size),
+            out_shape=jax.ShapeDtypeStruct((8, rows), jnp.float32),
+            in_specs=[hbm] * 4 + [vmem] * 3 + [smem] + [vmem] * 2,
+            out_specs=vmem,
+            scratch_shapes=[pltpu.VMEM((rows, rows), jnp.float32), pltpu.VMEM((1, rows), jnp.float32)]
+            + mlp_scratch_shapes(rows, model, ffn) + finish_scratch(dp_size),
+            compiler_params=pltpu.CompilerParams(collective_id=0, has_side_effects=True, vmem_limit_bytes=62 * 2**20),
+        )(x_blk[0], w_gate, w_up, w_down, norm_gain[None], final_gain[None], w_value[None], b_value[None], rew_blk, mask_blk)
+        row = jax.ShapeDtypeStruct((1, rows), jnp.float32)
+        return pl.pallas_call(hand_out, out_shape=(row, row, row), in_specs=[vmem], out_specs=(vmem,) * 3)(packed)
 
     tok_spec = P('dp', 'cp')
     in_specs = (P('dp', 'cp', None), P(None), P(None, None), P(None, None), P(None, None), P(None), P(None), P(), tok_spec, tok_spec)

time: 96.9 us -> 69.8 us (0.72)
  matrix products: 71.3 us -> 0 us
  Pallas kernels: 17.4 us -> 68.3 us
  local copies, waits for them, and re-layouts: 3.7 us -> 0 us
  other arithmetic: 2.86 us -> 0 us
    dot_general x3 -> x0, matrix products: 71.3 us -> none  [the longest x1 25 us: critic_values(): jnp.einsum('bsd,df->bsf', normed, w_gate, preferred_element_type=jnp.floa...]
    pallas_call x1 -> x2, Pallas kernels: 17.4 us -> 68.3 us  [the longest x1 67.1 us: local_step(): pl.pallas_call(functools.partial(kernel, dp_size), out_shape=jax.ShapeDty...]
    unnamed x11 -> x0, local copies, waits for them, and re-layouts: 3.7 us -> none
    reduce_sum x2 -> x0, other arithmetic: 2.27 us -> none  [the longest x1 1.8 us: critic_values(): jnp.mean(x_f32 * x_f32, axis=-1, keepdims=True) + NORM_EPS]
where the time goes in v2:
time: 69.8 us; the launch traced here: 69.6 us
  Pallas kernels  68.3 us (98%)
  between operations  1.29 us (2%)
    pallas_call x1, Pallas kernels, local_step(): pl.pallas_call(functools.partial(kernel, dp_size), out_shape=jax.ShapeDty...  67.1 us

profile of v2, /device:TPU:1, one launch (start us, length us, event | category | flops | bytes accessed | tf_op | source)
XLA Modules:
  0.0 69.6 jit_solution(15525336499694369257)
XLA Ops:
  1.3 67.1 %shard_map.121.packed_ref = f32[8,256]{1,0:T(8,128)} custom-call(bf16[256,3072]{1,0:T(8,128)(2,1)} %bitcast.6, bf16[3072,8192]{1,0:T(8,128)(2,1)} %wg.1, bf16[3072,8192]{1,0:T(8,128)(2,1)} %wu.1, bf16[8192,3072]{1,0:T(8,128)(2,1)} %wd.1, f32[1,3072]{1,0:T(1,128)} %bitcast.7, f32[1,3072]{1,0:T(1,128)} %bitcast.8, f32[1,3072]{1,0:T(1,128)} %bitcast.9, ...), custom_call_target="tpu_custom_call" | custom-call | tf_op jit(solution)/shard_map/pallas_call | solution.py:291
  68.3 1.3 %shard_map.122 = (f32[1,256]{1,0:T(1,128)}, f32[1,256]{1,0:T(1,128)}, f32[1,256]{1,0:T(1,128)}) custom-call(f32[8,256]{1,0:T(8,128)} %shard_map.121.packed_ref), custom_call_target="tpu_custom_call" | custom-call | tf_op jit(solution)/shard_map/pallas_call | solution.py:301

commit v3 on v1

v3 whole, which is shorter than its diff:
```python
import functools
import math

import jax
import jax.numpy as jnp
from jax import lax
from jax.experimental import pallas as pl
from jax.experimental.pallas import tpu as pltpu
from jax.sharding import PartitionSpec as P

NORM_EPS = 1e-6
WHITEN_EPS = 1e-8
DISCOUNT = 1.0
GAE_LAMBDA = 0.995
DECAY = DISCOUNT * GAE_LAMBDA
LOG_DECAY = math.log(DECAY)
MESH = pl.DeviceIdType.MESH


WIDE = 512
DEPTH2 = 2048
SLOTS = 3
AHEAD = 2
ALONE = 4


def silu_mul(g, u):
    return g * (1.0 / (1.0 + jnp.exp(-g))) * u


def dot(a, b):
    return jnp.dot(a, b, preferred_element_type=jnp.float32)


def mlp(dp_size, x_hbm, wg_hbm, wu_hbm, wd_hbm, g2_ref, gf_ref, wv_ref, rew_ref, mask_ref, weights_ref,
        x_buf, n_buf, n_stage, n_land, x_land, u_buf, u_stage, u_land, ring, h_buf, sq_acc, hd_acc, meta, meta_land,
        x_sem, ring_sem, n_send, n_recv, x_send, x_recv, meta_send, meta_recv, u_send, u_recv):
    rows, model = x_buf.shape
    ffn = u_buf.shape[1]
    chip, core = lax.axis_index("dp"), lax.axis_index("cp")
    chunks = ffn // WIDE
    shared = (chunks - ALONE) // 2
    out_cols = model // 2
    outs = out_cols // WIDE
    per_out = ffn // DEPTH2
    first2 = ALONE + shared
    steps = first2 + outs * per_out // 2

    def to_peer(src, dst, send, recv):
        return pltpu.make_async_remote_copy(src_ref=src, dst_ref=dst, send_sem=send, recv_sem=recv,
                                            device_id=(chip, 1 - core), device_id_type=MESH)

    def up_load(s, part, column):
        slot = lax.rem(s, SLOTS)
        src = (wg_hbm, wu_hbm)[part].at[:, pl.ds(pl.multiple_of(column * WIDE, WIDE), WIDE)]
        return pltpu.make_async_copy(src, ring.at[part, slot], ring_sem.at[part, slot])

    def column_at(s):
        if isinstance(s, int) and s < ALONE:
            return s
        return s + shared * core

    def down_load(s, part):
        slot = lax.rem(s, SLOTS)
        piece = (s - first2) * 2 + part
        o, j = piece // per_out, lax.rem(piece, per_out)
        src = wd_hbm.at[pl.ds(pl.multiple_of(depth_at(j) * DEPTH2, DEPTH2), DEPTH2),
                        pl.ds(pl.multiple_of(core * out_cols + o * WIDE, WIDE), WIDE)]
        return pltpu.make_async_copy(src, ring.at[part, slot, pl.ds(0, DEPTH2)], ring_sem.at[part, slot])

    def depth_at(j):
        turned = 1 + lax.rem(j + 2 + 2 * core, 3)
        if isinstance(j, int):
            return 0 if j == 0 else turned
        return jnp.where(j == 0, 0, turned)

    def start_load(s):
        for part in range(2):
            if s < first2:
                up_load(s, part, column_at(s)).start(priority=min(s, 1))
            else:
                down_load(s, part).start(priority=1)

    n_copy = to_peer(n_stage, n_land, n_send, n_recv)
    x_stage = n_stage.at[:, pl.ds(0, out_cols)]
    x_copy = to_peer(x_stage, x_land, x_send, x_recv)
    meta_copy = to_peer(meta, meta_land, meta_send, meta_recv)

    def u_copy(slot, unit):
        return to_peer(u_stage.at[slot], u_land.at[unit], u_send.at[slot], u_recv.at[unit])

    def take_unit(unit, block, column):
        u_copy(0, unit).wait_recv()
        u_buf[pl.ds(pl.multiple_of(block * rows, rows), rows), pl.ds(pl.multiple_of(column * WIDE, WIDE), WIDE)] = \
            u_land[unit].astype(jnp.bfloat16)

    own_x = pltpu.make_async_copy(x_hbm, x_buf, x_sem)
    own_x.start()
    for s in range(AHEAD):
        start_load(s)
    mask_row = mask_ref[...].astype(jnp.float32)
    meta[0:1, :] = reward_part(column_of(mask_row * rew_ref[...], rows), rows)
    meta[1:2, :] = mask_row
    weights_ref[...] = value_weights(rows)
    sq_acc[...] = jnp.zeros_like(sq_acc)
    hd_acc[...] = jnp.zeros_like(hd_acc)
    own_x.wait()

    def norm(b, _):
        r = pl.ds(pl.multiple_of(b * 32, 32), 32)
        xf = x_buf[r, :].astype(jnp.float32)
        scale = lax.rsqrt(jnp.mean(xf * xf, axis=1, keepdims=True) + NORM_EPS)
        normed = (xf * scale * g2_ref[...]).astype(jnp.bfloat16)
        n_buf[r, :] = normed
        n_stage[r, :] = normed.astype(jnp.float32)
        return 0

    lax.fori_loop(0, rows // 32, norm, 0)

    for s in range(ALONE):
        up_load(s, 0, column_at(s)).wait()
        start_load(s + AHEAD)
        gate = dot(n_buf[0:rows, :], ring[0, s % SLOTS])
        up_load(s, 1, column_at(s)).wait()
        hidden = silu_mul(gate, dot(n_buf[0:rows, :], ring[1, s % SLOTS])).astype(jnp.bfloat16)
        u_buf[0:rows, s * WIDE:(s + 1) * WIDE] = hidden
        u_stage[s] = hidden.astype(jnp.float32)
        if s == 0:
            await_greetings(dp_size)
            meta_copy.start()
            n_copy.start()
        u_copy(s, s).start()

    n_copy.wait_recv()
    n_buf[rows:2 * rows, :] = n_land[...].astype(jnp.bfloat16)
    n_copy.wait_send()
    x_stage[...] = x_buf[:, pl.ds(pl.multiple_of((1 - core) * out_cols, WIDE), out_cols)].astype(jnp.float32)
    x_copy.start()

    def both(b, _):
        for j in range(2):
            s = ALONE + 2 * b + j
            slot = lax.rem(s, SLOTS)
            column = column_at(s)
            for part in range(2):
                up_load(s, part, column).wait()
            @pl.when(s + AHEAD < first2)
            def _():
                for part in range(2):
                    up_load(s + AHEAD, part, column_at(s + AHEAD)).start(priority=1)

            @pl.when(s + AHEAD >= first2)
            def _():
                for part in range(2):
                    down_load(s + AHEAD, part).start(priority=1)
            for r in range(2):
                u_copy(2 * j + r, 0).wait_send()
            unit = 2 * b + j
            late = unit // ALONE
            take_unit(unit, 1 - lax.rem(unit, 2) * late, (1 - late) * unit + late * (ALONE + shared * (1 - core)))
            half = WIDE // 2
            for q in range(2):
                c = pl.ds(q * half, half)
                hidden = silu_mul(dot(n_buf[...], ring[0, slot, :, c]), dot(n_buf[...], ring[1, slot, :, c])).astype(jnp.bfloat16)
                u_buf[:, pl.ds(pl.multiple_of(column * WIDE + q * half, half), half)] = hidden
                wide = hidden.astype(jnp.float32)
                for r in range(2):
                    u_stage[2 * j + r, :, c] = wide[r * rows:(r + 1) * rows]
            for r in range(2):
                u_copy(2 * j + r, ALONE + 2 * (s - ALONE) + r).start()

        return 0

    lax.fori_loop(0, shared // 2, both, 0)

    def take_late(unit):
        take_unit(unit, 1 - unit % 2, ALONE + shared * (1 - core) + (unit - ALONE) // 2)

    def load_more(o, s):
        if isinstance(o, int):
            start_load(s)
        else:
            @pl.when(s < steps)
            def _():
                for part in range(2):
                    down_load(s, part).start(priority=1)

    def out_tile(o, starting):
        for j in range(per_out):
            s = first2 + 2 * o + j // 2
            slot, part = lax.rem(s, SLOTS), j % 2
            down_load(s, part).wait()
            if part == 0:
                load_more(o, s + AHEAD)
            if starting and j < 3:
                for unit in ((6, 7, 8, 9), (10, 11, 12, 13), (14, 15))[j]:
                    take_late(unit)
            if starting and j == 3:
                x_copy.wait_recv()
            lhs = u_buf[:, pl.ds(pl.multiple_of(depth_at(j) * DEPTH2, DEPTH2), DEPTH2)]
            if j < per_out - 1:
                value = dot(lhs, ring[part, slot, 0:DEPTH2])
                h_buf[...] = value if j == 0 else h_buf[...] + value
            else:
                half = WIDE // 2
                for q in range(2):
                    value = h_buf[:, q * half:(q + 1) * half] + dot(lhs, ring[part, slot, 0:DEPTH2, q * half:(q + 1) * half])
                    own = pl.ds(pl.multiple_of(core * out_cols + o * WIDE + q * half, half), half)
                    there = pl.ds(pl.multiple_of(o * WIDE + q * half, half), half)
                    head = gf_ref[:, own] * wv_ref[:, own]
                    for r, resid in enumerate((x_buf[:, own].astype(jnp.float32), x_land[:, there])):
                        block = slice(r * rows, (r + 1) * rows)
                        h = resid + value[block]
                        sq, hd = h * h, h * head
                        sq_acc[block, :] += sq[:, :128] + sq[:, 128:]
                        hd_acc[block, :] += hd[:, :128] + hd[:, 128:]

    out_tile(0, True)

    def rest(o, _):
        out_tile(o, False)
        return 0

    lax.fori_loop(1, outs, rest, 0)
    for slot in range(4):
        u_copy(slot, 0).wait_send()
    x_copy.wait_send()
    meta_copy.wait()


def greet(dp_size):
    chip, core = lax.axis_index("dp"), lax.axis_index("cp")
    barrier = pltpu.get_barrier_semaphore()
    pl.semaphore_signal(barrier, inc=1, device_id=(chip, 1 - core), device_id_type=MESH)

    def tell(k, _):
        pl.semaphore_signal(barrier, inc=1, device_id=(lax.rem(chip + k, dp_size), core), device_id_type=MESH)
        return 0

    lax.fori_loop(1, dp_size, tell, 0)


def await_greetings(dp_size):
    pl.semaphore_wait(pltpu.get_barrier_semaphore(), dp_size)


def positions(n):
    row = lax.broadcasted_iota(jnp.int32, (n, n), 0)
    col = lax.broadcasted_iota(jnp.int32, (n, n), 1)
    return row, col


def column_of(row_vec, n):
    row, col = positions(n)
    return jnp.sum(jnp.where(row == col, row_vec, 0.0), axis=1, keepdims=True)


def reward_part(rew_col, n):
    row, col = positions(n)
    gap = row - col
    decay = jnp.where(gap >= 0, jnp.exp(jnp.maximum(gap, 0).astype(jnp.float32) * LOG_DECAY), 0.0)
    return jnp.sum(decay * rew_col, axis=0, keepdims=True)


def value_weights(n):
    row, col = positions(n)
    gap = row - col
    later = DISCOUNT * (1.0 - GAE_LAMBDA) * jnp.exp(jnp.maximum(gap - 1, 0).astype(jnp.float32) * LOG_DECAY)
    return jnp.where(gap > 0, later, jnp.where(gap == 0, -1.0, 0.0))


def finish(dp_size, bv, model, weights_ref, sq_acc, hd_acc, meta, meta_land, out_ref,
           mine, theirs, total, gathered, pair_send, pair_recv, all_send, all_recv):
    n = meta.shape[1]
    chip, core = lax.axis_index("dp"), lax.axis_index("cp")
    row, col = positions(n)

    def to_row(col_vec):
        return jnp.sum(jnp.where(row == col, col_vec, 0.0), axis=0, keepdims=True)

    for r in range(2):
        block = slice(r * n, (r + 1) * n)
        mine[2 * r:2 * r + 1, :] = to_row(jnp.sum(sq_acc[block, :], axis=1, keepdims=True))
        mine[2 * r + 1:2 * r + 2, :] = to_row(jnp.sum(hd_acc[block, :], axis=1, keepdims=True))
    pair = pltpu.make_async_remote_copy(src_ref=mine, dst_ref=theirs, send_sem=pair_send, recv_sem=pair_recv,
                                        device_id=(chip, 1 - core), device_id_type=MESH)
    pair.start()
    own_mask, other_mask = meta[1:2, :], meta_land[1:2, :]
    is_left = core == 0
    ahead = (n - 1) - lax.broadcasted_iota(jnp.int32, (1, n), 1)
    reach = jnp.exp(ahead.astype(jnp.float32) * LOG_DECAY)
    pair.wait()

    def value(r, mask):
        square = mine[2 * r:2 * r + 1, :] + theirs[2 - 2 * r:3 - 2 * r, :]
        head = mine[2 * r + 1:2 * r + 2, :] + theirs[3 - 2 * r:4 - 2 * r, :]
        return mask * (head * lax.rsqrt(square * (1.0 / model) + NORM_EPS) + bv)

    own_v, other_v = value(0, own_mask), value(1, other_mask)
    weights = weights_ref[...]

    def local_adv(v, reward_row):
        return reward_row + jnp.sum(weights * column_of(v, n), axis=0, keepdims=True)

    own_adv, other_adv = local_adv(own_v, meta[0:1, :]), local_adv(other_v, meta_land[0:1, :])
    right_v = jnp.where(is_left, other_v, own_v)
    right_adv = jnp.where(is_left, other_adv, own_adv)
    carry = DISCOUNT * right_v[:, 0:1] + DECAY * right_adv[:, 0:1]
    own_adv = own_adv + jnp.where(is_left, carry, 0.0) * reach
    other_adv = other_adv + jnp.where(is_left, 0.0, carry) * reach
    own_m, other_m = own_mask * own_adv, other_mask * other_adv

    def add_up(a):
        return jnp.sum(a, axis=1, keepdims=True)

    parts = (add_up(own_mask + other_mask), add_up(own_m + other_m), add_up(own_m * own_adv + other_m * other_adv))
    lane = lax.broadcasted_iota(jnp.int32, (1, 128), 1)
    own = jnp.zeros((1, 128), jnp.float32)
    for place, part in enumerate(parts):
        own = jnp.where(lane == place, part, own)
    total[...] = own

    def push(k, _):
        pltpu.make_async_remote_copy(
            src_ref=total, dst_ref=gathered.at[pl.ds(k - 1, 1)], send_sem=all_send, recv_sem=all_recv,
            device_id=(lax.rem(chip + k, dp_size), core), device_id_type=MESH).start()
        return 0

    lax.fori_loop(1, dp_size, push, 0)
    out_ref[0:1, :] = own_v
    out_ref[1:2, :] = own_mask * (own_adv + own_v)
    everything = pltpu.make_async_remote_copy(src_ref=gathered, dst_ref=gathered, send_sem=all_send, recv_sem=all_recv,
                                              device_id=(chip, 1 - core), device_id_type=MESH)
    everything.wait_recv()
    sums = own + jnp.sum(gathered[...], axis=0, keepdims=True)
    count, first, second = sums[:, 0:1], sums[:, 1:2], sums[:, 2:3]
    mean = first / count
    var = second / count - mean * mean
    out_ref[2:3, :] = own_mask * (own_adv - mean) * lax.rsqrt(var + WHITEN_EPS)
    everything.wait_send()


def kernel(dp_size, x_hbm, wg, wu, wd, g2, gf, wv, bv, rew_ref, mask_ref, out_ref, weights_ref, *scratch):
    mlp_scratch, tail_scratch = scratch[:24], scratch[24:]
    greet(dp_size)
    mlp(dp_size, x_hbm, wg, wu, wd, g2, gf, wv, rew_ref, mask_ref, weights_ref, *mlp_scratch)
    finish(dp_size, bv[0], x_hbm.shape[1], weights_ref, *mlp_scratch[10:14], out_ref, *tail_scratch)


def hand_out(packed_ref, values_ref, returns_ref, white_ref):
    values_ref[...] = packed_ref[0:1, :]
    returns_ref[...] = packed_ref[1:2, :]
    white_ref[...] = packed_ref[2:3, :]


def scratch_shapes(dp_size, rows, model, ffn):
    bf, f32, sem = jnp.bfloat16, jnp.float32, pltpu.SemaphoreType.DMA
    vmem = pltpu.VMEM
    units = ALONE + (ffn // WIDE - ALONE)
    return [
        vmem((rows, rows), f32),
        vmem((rows, model), bf),
        vmem((2 * rows, model), bf),
        vmem((rows, model), f32),
        vmem((rows, model), f32),
        vmem((rows, model // 2), f32),
        vmem((2 * rows, ffn), bf),
        vmem((4, rows, WIDE), f32),
        vmem((units, rows, WIDE), f32),
        vmem((2, SLOTS, model, WIDE), bf),
        vmem((2 * rows, WIDE), f32),
        vmem((2 * rows, 128), f32),
        vmem((2 * rows, 128), f32),
        vmem((8, rows), f32),
        vmem((8, rows), f32),
        sem, sem((2, SLOTS)), sem, sem, sem, sem, sem, sem, sem((4,)), sem((units,)),
        vmem((8, rows), f32),
        vmem((8, rows), f32),
        vmem((1, 128), f32),
        vmem((dp_size - 1, 128), f32),
        sem, sem, sem, sem,
    ]


def solution(mesh):
    dp_size = mesh.shape['dp']

    def local_step(x_blk, norm_gain, w_gate, w_up, w_down, final_gain, w_value, b_value, rew_blk, mask_blk):
        rows = rew_blk.shape[1]
        model, ffn = w_gate.shape
        hbm = pl.BlockSpec(memory_space=pl.ANY)
        vmem = pl.BlockSpec(memory_space=pltpu.VMEM)
        smem = pl.BlockSpec(memory_space=pltpu.SMEM)
        packed = pl.pallas_call(
            functools.partial(kernel, dp_size),
            out_shape=jax.ShapeDtypeStruct((8, rows), jnp.float32),
            in_specs=[hbm] * 4 + [vmem] * 3 + [smem] + [vmem] * 2,
            out_specs=vmem,
            scratch_shapes=scratch_shapes(dp_size, rows, model, ffn),
            compiler_params=pltpu.CompilerParams(collective_id=0, has_side_effects=True, vmem_limit_bytes=63 * 2**20),
        )(x_blk[0], w_gate, w_up, w_down, norm_gain[None], final_gain[None], w_value[None], b_value[None], rew_blk, mask_blk)
        row = jax.ShapeDtypeStruct((1, rows), jnp.float32)
        return pl.pallas_call(hand_out, out_shape=(row, row, row), in_specs=[vmem], out_specs=(vmem,) * 3)(packed)

    tok_spec = P('dp', 'cp')
    in_specs = (P('dp', 'cp', None), P(None), P(None, None), P(None, None), P(None, None), P(None), P(None), P(), tok_spec, tok_spec)
    return jax.shard_map(local_step, mesh=mesh, in_specs=in_specs, out_specs=(tok_spec, tok_spec, tok_spec), check_vma=False)
```

time: 96.9 us -> 67.8 us (0.70)
  matrix products: 71.3 us -> 0 us
  Pallas kernels: 17.4 us -> 66.3 us
  local copies, waits for them, and re-layouts: 3.7 us -> 0 us
  other arithmetic: 2.86 us -> 0 us
    dot_general x3 -> x0, matrix products: 71.3 us -> none  [the longest x1 25 us: critic_values(): jnp.einsum('bsd,df->bsf', normed, w_gate, preferred_element_type=jnp.floa...]
    pallas_call x1 -> x2, Pallas kernels: 17.4 us -> 66.3 us  [the longest x1 65 us: local_step(): pl.pallas_call(functools.partial(kernel, dp_size), out_shape=jax.ShapeDty...]
    unnamed x11 -> x0, local copies, waits for them, and re-layouts: 3.7 us -> none
    reduce_sum x2 -> x0, other arithmetic: 2.27 us -> none  [the longest x1 1.8 us: critic_values(): jnp.mean(x_f32 * x_f32, axis=-1, keepdims=True) + NORM_EPS]
where the time goes in v3:
time: 67.8 us; the launch traced here: 67.5 us
  Pallas kernels  66.3 us (98%)
  between operations  1.29 us (2%)
    pallas_call x1, Pallas kernels, local_step(): pl.pallas_call(functools.partial(kernel, dp_size), out_shape=jax.ShapeDty...  65 us

profile of v3, /device:TPU:1, one launch (start us, length us, event | category | flops | bytes accessed | tf_op | source)
XLA Modules:
  0.0 67.5 jit_solution(11441757269456083417)
XLA Ops:
  1.3 65.0 %shard_map.121.packed_ref = f32[8,256]{1,0:T(8,128)} custom-call(bf16[256,3072]{1,0:T(8,128)(2,1)} %bitcast.6, bf16[3072,8192]{1,0:T(8,128)(2,1)} %wg.1, bf16[3072,8192]{1,0:T(8,128)(2,1)} %wu.1, bf16[8192,3072]{1,0:T(8,128)(2,1)} %wd.1, f32[1,3072]{1,0:T(1,128)} %bitcast.7, f32[1,3072]{1,0:T(1,128)} %bitcast.8, f32[1,3072]{1,0:T(1,128)} %bitcast.9, ...), custom_call_target="tpu_custom_call" | custom-call | tf_op jit(solution)/shard_map/pallas_call | solution.py:394
  66.3 1.3 %shard_map.122 = (f32[1,256]{1,0:T(1,128)}, f32[1,256]{1,0:T(1,128)}, f32[1,256]{1,0:T(1,128)}) custom-call(f32[8,256]{1,0:T(8,128)} %shard_map.121.packed_ref), custom_call_target="tpu_custom_call" | custom-call | tf_op jit(solution)/shard_map/pallas_call | solution.py:403

commit v4 on v3

--- a/solution.py
+++ b/solution.py
@@ -21,6 +21,10 @@
 DEPTH2 = 2048
 SLOTS = 3
 AHEAD = 2
+SPLIT = 1
+SPLIT2 = 1
+FIRST = 1
+EAGER = 2
 ALONE = 4
 
 
@@ -50,23 +54,23 @@
         return pltpu.make_async_remote_copy(src_ref=src, dst_ref=dst, send_sem=send, recv_sem=recv,
                                             device_id=(chip, 1 - core), device_id_type=MESH)
 
-    def up_load(s, part, column):
-        slot = lax.rem(s, SLOTS)
-        src = (wg_hbm, wu_hbm)[part].at[:, pl.ds(pl.multiple_of(column * WIDE, WIDE), WIDE)]
-        return pltpu.make_async_copy(src, ring.at[part, slot], ring_sem.at[part, slot])
+    def up_load(s, part, column, rows_from=0, row_count=model):
+        slot, r = lax.rem(s, SLOTS), pl.ds(rows_from, row_count)
+        src = (wg_hbm, wu_hbm)[part].at[r, pl.ds(pl.multiple_of(column * WIDE, WIDE), WIDE)]
+        return pltpu.make_async_copy(src, ring.at[part, slot, r], ring_sem.at[part, slot])
 
     def column_at(s):
         if isinstance(s, int) and s < ALONE:
             return s
         return s + shared * core
 
-    def down_load(s, part):
+    def down_load(s, part, rows_from=0, row_count=DEPTH2):
         slot = lax.rem(s, SLOTS)
         piece = (s - first2) * 2 + part
         o, j = piece // per_out, lax.rem(piece, per_out)
-        src = wd_hbm.at[pl.ds(pl.multiple_of(depth_at(j) * DEPTH2, DEPTH2), DEPTH2),
+        src = wd_hbm.at[pl.ds(pl.multiple_of(depth_at(j) * DEPTH2 + rows_from, row_count), row_count),
                         pl.ds(pl.multiple_of(core * out_cols + o * WIDE, WIDE), WIDE)]
-        return pltpu.make_async_copy(src, ring.at[part, slot, pl.ds(0, DEPTH2)], ring_sem.at[part, slot])
+        return pltpu.make_async_copy(src, ring.at[part, slot, pl.ds(rows_from, row_count)], ring_sem.at[part, slot])
 
     def depth_at(j):
         turned = 1 + lax.rem(j + 2 + 2 * core, 3)
@@ -74,12 +78,21 @@
             return 0 if j == 0 else turned
         return jnp.where(j == 0, 0, turned)
 
+    def start_up(s):
+        for part in range(2):
+            for i in range(SPLIT):
+                up_load(s, part, column_at(s), i * (model // SPLIT), model // SPLIT).start(priority=FIRST)
+
+    def start_down(s):
+        for part in range(2):
+            for i in range(SPLIT2):
+                down_load(s, part, i * (DEPTH2 // SPLIT2), DEPTH2 // SPLIT2).start(priority=FIRST)
+
     def start_load(s):
-        for part in range(2):
-            if s < first2:
-                up_load(s, part, column_at(s)).start(priority=min(s, 1))
-            else:
-                down_load(s, part).start(priority=1)
+        if s < first2:
+            start_up(s)
+        else:
+            start_down(s)
 
     n_copy = to_peer(n_stage, n_land, n_send, n_recv)
     x_stage = n_stage.at[:, pl.ds(0, out_cols)]
@@ -96,7 +109,7 @@
 
     own_x = pltpu.make_async_copy(x_hbm, x_buf, x_sem)
     own_x.start()
-    for s in range(AHEAD):
+    for s in range(EAGER):
         start_load(s)
     mask_row = mask_ref[...].astype(jnp.float32)
     meta[0:1, :] = reward_part(column_of(mask_row * rew_ref[...], rows), rows)
@@ -117,24 +130,26 @@
 
     lax.fori_loop(0, rows // 32, norm, 0)
 
+    await_greetings(dp_size)
+    meta_copy.start()
+    n_copy.start()
+
     for s in range(ALONE):
         up_load(s, 0, column_at(s)).wait()
-        start_load(s + AHEAD)
+        if s + AHEAD >= EAGER:
+            start_load(s + AHEAD)
         gate = dot(n_buf[0:rows, :], ring[0, s % SLOTS])
         up_load(s, 1, column_at(s)).wait()
+        if s == ALONE - 1:
+            n_copy.wait_recv()
+            n_buf[rows:2 * rows, :] = n_land[...].astype(jnp.bfloat16)
+            n_copy.wait_send()
+            x_stage[...] = x_buf[:, pl.ds(pl.multiple_of((1 - core) * out_cols, WIDE), out_cols)].astype(jnp.float32)
         hidden = silu_mul(gate, dot(n_buf[0:rows, :], ring[1, s % SLOTS])).astype(jnp.bfloat16)
         u_buf[0:rows, s * WIDE:(s + 1) * WIDE] = hidden
         u_stage[s] = hidden.astype(jnp.float32)
-        if s == 0:
-            await_greetings(dp_size)
-            meta_copy.start()
-            n_copy.start()
         u_copy(s, s).start()
 
-    n_copy.wait_recv()
-    n_buf[rows:2 * rows, :] = n_land[...].astype(jnp.bfloat16)
-    n_copy.wait_send()
-    x_stage[...] = x_buf[:, pl.ds(pl.multiple_of((1 - core) * out_cols, WIDE), out_cols)].astype(jnp.float32)
     x_copy.start()
 
     def both(b, _):
@@ -146,13 +161,11 @@
                 up_load(s, part, column).wait()
             @pl.when(s + AHEAD < first2)
             def _():
-                for part in range(2):
-                    up_load(s + AHEAD, part, column_at(s + AHEAD)).start(priority=1)
+                start_up(s + AHEAD)
 
             @pl.when(s + AHEAD >= first2)
             def _():
-                for part in range(2):
-                    down_load(s + AHEAD, part).start(priority=1)
+                start_down(s + AHEAD)
             for r in range(2):
                 u_copy(2 * j + r, 0).wait_send()
             unit = 2 * b + j
@@ -176,22 +189,13 @@
     def take_late(unit):
         take_unit(unit, 1 - unit % 2, ALONE + shared * (1 - core) + (unit - ALONE) // 2)
 
-    def load_more(o, s):
-        if isinstance(o, int):
-            start_load(s)
-        else:
-            @pl.when(s < steps)
-            def _():
-                for part in range(2):
-                    down_load(s, part).start(priority=1)
-
     def out_tile(o, starting):
         for j in range(per_out):
             s = first2 + 2 * o + j // 2
             slot, part = lax.rem(s, SLOTS), j % 2
             down_load(s, part).wait()
-            if part == 0:
-                load_more(o, s + AHEAD)
+            if part == 0 and s + AHEAD < steps:
+                start_load(s + AHEAD)
             if starting and j < 3:
                 for unit in ((6, 7, 8, 9), (10, 11, 12, 13), (14, 15))[j]:
                     take_late(unit)
@@ -215,13 +219,8 @@
                         sq_acc[block, :] += sq[:, :128] + sq[:, 128:]
                         hd_acc[block, :] += hd[:, :128] + hd[:, 128:]
 
-    out_tile(0, True)
-
-    def rest(o, _):
-        out_tile(o, False)
-        return 0
-
-    lax.fori_loop(1, outs, rest, 0)
+    for o in range(outs):
+        out_tile(o, o == 0)
     for slot in range(4):
         u_copy(slot, 0).wait_send()
     x_copy.wait_send()
@@ -267,6 +266,17 @@
     gap = row - col
     later = DISCOUNT * (1.0 - GAE_LAMBDA) * jnp.exp(jnp.maximum(gap - 1, 0).astype(jnp.float32) * LOG_DECAY)
     return jnp.where(gap > 0, later, jnp.where(gap == 0, -1.0, 0.0))
+
+
+def others(chip, dp_size):
+    side = round(dp_size ** (1 / 3))
+    if side ** 3 != dp_size:
+        return [lax.rem(chip + k, dp_size) for k in range(1, dp_size)]
+    coords = [lax.rem(chip // side ** i, side) for i in range(3)]
+    shifted = [[lax.rem(c + d, side) * side ** i for d in range(side)] for i, c in enumerate(coords)]
+    steps = sorted(((min(x, side - x) + min(y, side - y) + min(z, side - z)), x, y, z)
+                   for x in range(side) for y in range(side) for z in range(side))
+    return [shifted[0][x] + shifted[1][y] + shifted[2][z] for _, x, y, z in steps[:0:-1]]
 
 
 def finish(dp_size, bv, model, weights_ref, sq_acc, hd_acc, meta, meta_land, out_ref,
@@ -320,13 +330,10 @@
         own = jnp.where(lane == place, part, own)
     total[...] = own
 
-    def push(k, _):
+    for k, there in enumerate(others(chip, dp_size)):
         pltpu.make_async_remote_copy(
-            src_ref=total, dst_ref=gathered.at[pl.ds(k - 1, 1)], send_sem=all_send, recv_sem=all_recv,
-            device_id=(lax.rem(chip + k, dp_size), core), device_id_type=MESH).start()
-        return 0
-
-    lax.fori_loop(1, dp_size, push, 0)
+            src_ref=total, dst_ref=gathered.at[pl.ds(k, 1)], send_sem=all_send, recv_sem=all_recv,
+            device_id=(there, core), device_id_type=MESH).start()
     out_ref[0:1, :] = own_v
     out_ref[1:2, :] = own_mask * (own_adv + own_v)
     everything = pltpu.make_async_remote_copy(src_ref=gathered, dst_ref=gathered, send_sem=all_send, recv_sem=all_recv,

time: 67.8 us -> 64.9 us (0.957)
  Pallas kernels: 66.3 us -> 63.4 us
    pallas_call x1, Pallas kernels: 65 us -> 62.2 us  [local_step(): pl.pallas_call(functools.partial(kernel, dp_size), out_shape=jax.ShapeDty...]
where the time goes in v4:
time: 64.9 us; the launch traced here: 64.7 us
  Pallas kernels  63.4 us (98%)
  between operations  1.29 us (2%)
    pallas_call x1, Pallas kernels, local_step(): pl.pallas_call(functools.partial(kernel, dp_size), out_shape=jax.ShapeDty...  62.2 us

profile of v4, /device:TPU:1, one launch (start us, length us, event | category | flops | bytes accessed | tf_op | source)
XLA Modules:
  0.0 64.7 jit_solution(17300644921522128820)
XLA Ops:
  1.3 62.2 %shard_map.121.packed_ref = f32[8,256]{1,0:T(8,128)} custom-call(bf16[256,3072]{1,0:T(8,128)(2,1)} %bitcast.6, bf16[3072,8192]{1,0:T(8,128)(2,1)} %wg.1, bf16[3072,8192]{1,0:T(8,128)(2,1)} %wu.1, bf16[8192,3072]{1,0:T(8,128)(2,1)} %wd.1, f32[1,3072]{1,0:T(1,128)} %bitcast.7, f32[1,3072]{1,0:T(1,128)} %bitcast.8, f32[1,3072]{1,0:T(1,128)} %bitcast.9, ...), custom_call_target="tpu_custom_call" | custom-call | tf_op jit(solution)/shard_map/pallas_call | solution.py:401
  63.5 1.3 %shard_map.122 = (f32[1,256]{1,0:T(1,128)}, f32[1,256]{1,0:T(1,128)}, f32[1,256]{1,0:T(1,128)}) custom-call(f32[8,256]{1,0:T(8,128)} %shard_map.121.packed_ref), custom_call_target="tpu_custom_call" | custom-call | tf_op jit(solution)/shard_map/pallas_call | solution.py:410
